TPU v7x, 128 devices: a whole 4x4x4 slice. The times are simulated.
128 devices in a mesh: seq: 4 (over x), head: 32 (over y, z, core).
Axes of the slice: x: 4, y: 4, z: 4, core: 2. Of those that a mesh axis runs over, the one named last changes fastest.
Arguments:
- queries: bfloat16 [32768, 4096], P(('seq', 'head')), may hold values from -6 to 6
- key_vectors: bfloat16 [32768, 4096], P(('seq', 'head')), may hold values from -0.375 to 0.375
- values: bfloat16 [32768, 8192], P(('seq', 'head')), may hold values from -6 to 6
- decay_log: bfloat16 [32768, 16], P(('seq', 'head')), may hold values from -0.8 to 0, as said below
- gate_input: bfloat16 [32768, 8192], P(('seq', 'head')), may hold values from -6 to 6
Outputs:
- retention_out: bfloat16 [32768, 8192], P(('seq', 'head'))
Inputs may be any that keep to these rules, and one draw needn't show every extreme that they name: `decay_log`: every entry is negative.
All inputs are finite; a program needn't handle non-finite values.
Results may differ from a plain program's by a relative error of at most 0.0063.
Values may be sent and summed in bfloat16 or wider, within the bound.
A program may use at most 128 MiB of HBM per device.

v0:
```python
import math

import jax
import jax.numpy as jnp
from jax import lax
from jax.sharding import PartitionSpec as P

BLOCK = 512


def sent_to_all(shard, axis):
    count = lax.axis_size(axis)
    return lax.all_to_all(
        jnp.broadcast_to(shard[None], (count, *shard.shape)), axis, 0, 0, tiled=True
    )


def laid_out(tiles, dim):
    tiles = jnp.moveaxis(tiles, 0, dim)
    dims = tiles.shape
    return tiles.reshape(*dims[:dim], dims[dim] * dims[dim + 1], *dims[dim + 2 :])


def gather_directly(shard, axis, dim):
    tiles = sent_to_all(shard, axis)
    return laid_out(tiles, dim)


def sent_together(arrays, axis, dim, along):
    widths = [math.prod(a.shape[along:]) for a in arrays]
    both = jnp.concatenate(
        [a.reshape(*a.shape[:along], w) for a, w in zip(arrays, widths)], axis=along
    )
    result = gather_directly(both, axis, dim)
    tiles = jnp.split(result, [sum(widths[:k]) for k in range(1, len(widths))], axis=along)
    return tuple(
        (b.reshape(*result.shape[:along], *a.shape[along:]) for a, b in zip(arrays, tiles))
    )


def cut_along(shard, dim, count):
    before, after = (shard.shape[:dim], shard.shape[dim + 1 :])
    return jnp.moveaxis(shard.reshape(*before, count, -1, *after), dim, 0)


def cut_rows(length, count):
    unit = 8 if length >= 8 * count else 1
    return [length // unit * k // count * unit for k in range(1, count)]


def exchange_in_pieces(shard, axis, pieces, split_dim, concat_dim):
    tiles = cut_along(shard, split_dim, lax.axis_size(axis))
    cut = max(range(1, max(2, tiles.ndim - 1)), key=lambda d: tiles.shape[d])
    done = []
    for piece in jnp.split(tiles, cut_rows(tiles.shape[cut], pieces), axis=cut):
        if piece.size:
            done.append(lax.all_to_all(piece, axis, split_axis=0, concat_axis=0, tiled=True))
    return laid_out(jnp.concatenate(done, axis=cut), concat_dim)


def side_by_side(arrays, axis, split_dim, concat_dim, along):
    columns = [a.reshape(*a.shape[:along], -1) for a in arrays]
    both = jnp.concatenate(columns, axis=along)
    result, at, done = (
        lax.all_to_all(both, axis, split_axis=split_dim, concat_axis=concat_dim, tiled=True),
        0,
        [],
    )
    for a, column in zip(arrays, columns):
        piece = result[..., at : at + column.shape[along]]
        done.append(piece.reshape(*piece.shape[:along], *a.shape[along:]))
        at += column.shape[along]
    return tuple(done)


def partner_2(value, axis, apart):
    mask = 2**apart
    pairs = [(source, source ^ mask) for source in range(lax.axis_size(axis))]
    return lax.ppermute(value, axis, pairs)


def prefix_state(damping, closing):
    gathered = sent_together((damping[None], closing[None]), "seq", 0, 2)
    my_index = lax.axis_index("seq")

    def absorb(source, running_state):
        rate_row = lax.dynamic_index_in_dim(gathered[0], source, 0, keepdims=False)
        state_row = lax.dynamic_index_in_dim(gathered[1], source, 0, keepdims=False)
        stepped = rate_row[:, None, None] * running_state + state_row
        return jnp.where(source < my_index, stepped, running_state)

    incoming = lax.fori_loop(0, lax.axis_size("seq"), absorb, jnp.zeros_like(closing))
    return incoming


def retain_items(query_part, key_part, value_part, decay_part, carry_in):
    length, count, key_width = query_part.shape
    width = value_part.shape[2]
    blocks = length // BLOCK
    running = jnp.cumsum(decay_part.astype(jnp.float32).reshape(blocks, BLOCK, count), axis=1)
    block_decay = running[:, -1, :]
    query_blocks = query_part.reshape(blocks, BLOCK, count, key_width)
    key_blocks = key_part.reshape(blocks, BLOCK, count, key_width)
    value_blocks = value_part.reshape(blocks, BLOCK, count, width)
    faded = (
        key_blocks.astype(jnp.float32) * jnp.exp(block_decay[:, None, :] - running)[..., None]
    ).astype(jnp.bfloat16)
    additions = jnp.einsum(
        "bjnd,bjnw->bndw", faded, value_blocks, preferred_element_type=jnp.float32
    )

    def advance(carried_state, pieces):
        rate_row, addition = pieces
        return (jnp.exp(rate_row)[:, None, None] * carried_state + addition, carried_state)

    initial = jnp.zeros((count, key_width, width), jnp.float32)
    closing, local_starts = lax.scan(advance, initial, (block_decay, additions))
    damping = jnp.exp(jnp.sum(block_decay, axis=0))
    incoming = carry_in(damping, closing)
    before = jnp.cumsum(block_decay, axis=0) - block_decay
    starts = local_starts + jnp.exp(before)[:, :, None, None] * incoming[None]
    causal = jnp.arange(BLOCK)[:, None] >= jnp.arange(BLOCK)[None, :]

    def emit_block(pieces):
        query_block, key_block, value_block, running_block, start_state = pieces
        scores = jnp.einsum(
            "ind,jnd->nij", query_block, key_block, preferred_element_type=jnp.float32
        )
        spread = running_block.T[:, :, None] - running_block.T[:, None, :]
        factor = jnp.exp(jnp.where(causal[None], spread, -jnp.inf))
        weights = (scores * factor).astype(jnp.bfloat16)
        within = jnp.einsum(
            "nij,jnw->inw", weights, value_block, preferred_element_type=jnp.float32
        )
        across = jnp.einsum(
            "ind,ndw->inw",
            query_block,
            start_state.astype(jnp.bfloat16),
            preferred_element_type=jnp.float32,
        )
        across = across * jnp.exp(running_block)[:, :, None]
        return (within + across).astype(jnp.bfloat16)

    retained = lax.map(emit_block, (query_blocks, key_blocks, value_blocks, running, starts))
    return retained.reshape(length, count, width)


def send_back(retained):
    return exchange_in_pieces(retained[:, None], "head", 2, 0, 1)


def shards(queries, key_vectors, values, decay_log, gate_input):
    rows_here = queries.shape[0]
    head_count = decay_log.shape[1]
    key_width = queries.shape[1] // head_count
    value_width = values.shape[1] // head_count
    half_width = value_width // 2
    groups = lax.axis_size("head")
    per_device = 2 * head_count // groups
    value_items = values.reshape(rows_here, groups, per_device, half_width)
    decay_items = jnp.repeat(decay_log, 2, axis=1).reshape(rows_here, groups, per_device)
    paired = jnp.stack(
        (
            queries.reshape(rows_here, head_count, key_width),
            key_vectors.reshape(rows_here, head_count, key_width),
        ),
        axis=2,
    )
    paired = paired.reshape(rows_here, groups, per_device, key_width)
    paired_got, value_got, decay_got = side_by_side(
        (paired, value_items, decay_items), "head", 1, 0, 3
    )
    paired_got = paired_got[:, 0]
    value_got = value_got[:, 0]
    decay_got = decay_got[:, 0]
    length = paired_got.shape[0]
    partner = partner_2(paired_got, "head", 0)
    is_first = lax.axis_index("head") % 2 == 0
    query_sel = jnp.where(is_first, paired_got, partner)
    key_sel = jnp.where(is_first, partner, paired_got)
    retained = retain_items(query_sel, key_sel, value_got, decay_got, prefix_state)
    gathered_out = send_back(retained)
    retained_all = gathered_out.reshape(rows_here, head_count, value_width).astype(jnp.float32)
    average = jnp.mean(retained_all, axis=2, keepdims=True)
    centered = retained_all - average
    variance = jnp.mean(centered * centered, axis=2, keepdims=True)
    normed = centered / jnp.sqrt(variance + 1e-06)
    gated = (
        jax.nn.silu(gate_input.astype(jnp.float32).reshape(rows_here, head_count, value_width))
        * normed
    )
    return gated.astype(jnp.bfloat16).reshape(rows_here, head_count * value_width)


def solution(mesh):
    in_specs = (
        P(("seq", "head"), None),
        P(("seq", "head"), None),
        P(("seq", "head"), None),
        P(("seq", "head"), None),
        P(("seq", "head"), None),
    )
    out_specs = P(("seq", "head"), None)
    return jax.shard_map(shards, mesh=mesh, in_specs=in_specs, out_specs=out_specs, check_vma=False)
```

profile of v0, /device:TPU:1, one launch (start us, length us, event | category | flops | bytes accessed | tf_op | source)
XLA Modules:
  0.0 395.2 jit_solution(3180133201213793007)
XLA Ops:
  0.0 3.3 copy.95
  3.3 4.1 %copy.96 = bf16[256,4096]{0,1:T(8,128)(2,1)} copy(bf16[256,4096]{1,0:T(8,128)(2,1)} %param.12) | data formatting | bytes 4194304 | tf_op jit(solution)/shard_map/stack;reshape | solution.py:162
  7.4 6.4 %copy.74 = bf16[256,8192]{0,1:T(8,128)(2,1)} copy(bf16[256,8192]{1,0:T(8,128)(2,1)} %param.13) | data formatting | bytes 8388608 | tf_op args[2]
  13.8 2.1 pad_maximum_fusion.1
  17.2 107.1 %all_to_all.33 = bf16[256,32,1,513]{0,3,2,1:T(8,128)(2,1)} all-to-all(bf16[256,32,1,513]{0,3,2,1:T(8,128)(2,1)S(1)} %pad_maximum_fusion), channel_id=1, replica_groups=mesh['seq'=4,'head'=32] {'head'}, dimensions={1} | all-to-all | bytes 16809984 | tf_op jit(solution)/shard_map/all_to_all | solution.py:65
  124.3 13.5 %copy.76 = bf16[32,256,1,1,513]{4,1,0,3,2:T(8,128)(2,1)} copy(bf16[32,256,1,1,513]{1,4,0,3,2:T(8,128)(2,1)} %bitcast.175) | data formatting | bytes 16809984 | tf_op jit(solution)/shard_map/all_to_all | solution.py:65
  137.8 5.9 %slice_bitcast_fusion = (bf16[8192,1,256]{2,0,1:T(8,128)(2,1)}, bf16[8192,1,1,256]{3,0,2,1:T(8,128)(2,1)}) fusion(bf16[8192,1,1,513]{3,0,2,1:T(8,128)(2,1)} %bitcast.172), kind=kLoop, calls=%fused_computation.54 | loop fusion | bytes 16777216 | tf_op jit(solution)/shard_map/squeeze | solution.py:173
  144.1 2.2 convert_reduce_fusion
  149.6 1.6 collective-permute-done
  151.2 5.1 %broadcast_select_fusion = (bf16[8192,1,256]{2,0,1:T(8,128)(2,1)S(1)}, bf16[8192,1,256]{2,0,1:T(8,128)(2,1)}) fusion(bf16[8192,1,256]{2,0,1:T(8,128)(2,1)} %collective-permute-done, pred[]{:T(512)S(6)} %eq.5, bf16[8192,1,1,513]{3,0,2,1:T(8,128)(2,1)} %bitcast.174), kind=kLoop, calls=%fused_computation.60 | loop fusion | flops 4194304 | bytes 16777216 | tf_op jit(solution)/shard_map/jit(_where)/select_n | solution.py:180
  156.3 4.3 %fusion.44 = f32[16,1,256,256]{3,2,1,0:T(8,128)} fusion(bf16[16,512,256]{2,1,0:T(8,128)(2,1)S(1)} %bitcast.179, bf16[16,512,256]{2,1,0:T(8,128)(2,1)S(1)} %bitcast.176, f32[16,512]{1,0:T(8,128)S(1)} %fusion.48), kind=kOutput, calls=%fused_computation.62 | convolution fusion | flops 1080033280 | bytes 12615680 | tf_op jit(solution)/shard_map/bjnd,bjnw->bndw/dot_general | solution.py:108
  160.6 48.5 %while.39 = (s32[]{:T(128)}, f32[1,256,256]{2,1,0:T(8,128)S(1)}, f32[16,1,256,256]{3,2,1,0:T(8,128)}, f32[16,1]{0,1:T(1,128)S(1)}, f32[16,1,256,256]{3,2,1,0:T(8,128)}, /*index=5*/s32[]{:T(128)}, s32[]{:T(128)}) while((s32[]{:T(128)}, f32[1,256,256]{2,1,0:T(8,128)S(1)}, f32[16,1,256,256]{3,2,1,0:T(8,128)}, f32[16,1]{0,1:T(1,128)S(1)}, ...), condition=%wide.region_3.4_spmd.clone, body=%wide.region_2.3_spmd.clone.sunk | while | flops 262147 | bytes 1311340 | solution.py:117
  162.0 1.7 bitcast_add_fusion.4
  165.0 1.7 bitcast_add_fusion.4
  168.0 1.7 bitcast_add_fusion.4
  171.1 1.7 bitcast_add_fusion.4
  174.1 1.7 bitcast_add_fusion.4
  177.1 1.7 bitcast_add_fusion.4
  180.2 1.7 bitcast_add_fusion.4
  183.2 1.7 bitcast_add_fusion.4
  186.2 1.7 bitcast_add_fusion.4
  189.2 1.7 bitcast_add_fusion.4
  192.3 1.7 bitcast_add_fusion.4
  195.3 1.7 bitcast_add_fusion.4
  198.3 1.7 bitcast_add_fusion.4
  201.4 1.7 bitcast_add_fusion.4
  204.4 1.7 bitcast_add_fusion.4
  207.4 1.7 bitcast_add_fusion.4
  210.1 1.5 broadcast_in_dim.46
  211.6 4.0 %all-to-all-start.1 = ((f32[4,1,1,65537]{3,2,1,0:T(1,128)}), f32[4,1,1,65537]{3,2,1,0:T(1,128)S(1)}, u32[]{:S(2)}, u32[]{:S(2)}) async-start(f32[4,1,1,65537]{3,2,1,0:T(1,128)} %broadcast_in_dim.46), calls=%async_computation.1 | async-start | bytes 2101248 | tf_op jit(solution)/shard_map/all_to_all | solution.py:13
  215.8 14.4 %all-to-all-done.1 = f32[4,1,1,65537]{3,2,1,0:T(1,128)S(1)} async-done(((f32[4,1,1,65537]{3,2,1,0:T(1,128)}), f32[4,1,1,65537]{3,2,1,0:T(1,128)S(1)}, u32[]{:S(2)}, u32[]{:S(2)}) %all-to-all-start.1) | async-done | bytes 1048624 | tf_op jit(solution)/shard_map/all_to_all | solution.py:13
  230.2 3.4 slice_reduce_fusion
  233.9 5.8 %while.40 = (s32[]{:T(128)}, f32[1,256,256]{2,1,0:T(8,128)S(1)}, s32[]{:T(128)}, f32[4,1]{0,1:T(1,128)S(1)}, f32[4,1,256,256]{3,2,1,0:T(8,128)S(1)}, /*index=5*/s32[]{:T(128)}, s32[]{:T(128)}) while((s32[]{:T(128)}, f32[1,256,256]{2,1,0:T(8,128)S(1)}, s32[]{:T(128)}, f32[4,1]{0,1:T(1,128)S(1)}, f32[4,1,256,256]{3,2,1,0:T(8,128)S(1)}, ...), condition=%wide.region_7.8_spmd.clone, body=%wide.region_6.7_spmd.clone.sunk | while | flops 262148 | bytes 786549 | solution.py:92
  239.7 2.7 multiply_add_fusion
  242.4 61.1 %while.38 = (s32[]{:T(128)}, bf16[16,512,1,256]{3,1,0,2:T(8,128)(2,1)}, bf16[16,512,1,256]{3,1,2,0:T(8,128)(2,1)}, bf16[16,512,1,256]{3,1,2,0:T(8,128)(2,1)}, bf...) while((s32[]{:T(128)}, ...), condition=%wide.region_9.10_spmd.clone, body=%wide.region_8.9_spmd.clone.sunk | while | flops 337248256 | bytes 3556441 | solution.py:144
  242.5 1.7 convolution_bitcast_fusion.3
  244.2 1.2 fusion.64
  246.3 1.7 convolution_bitcast_fusion.3
  250.1 1.7 convolution_bitcast_fusion.3
  253.9 1.7 convolution_bitcast_fusion.3
  257.8 1.7 convolution_bitcast_fusion.3
  261.6 1.7 convolution_bitcast_fusion.3
  265.4 1.7 convolution_bitcast_fusion.3
  269.2 1.7 convolution_bitcast_fusion.3
  273.0 1.7 convolution_bitcast_fusion.3
  276.8 1.7 convolution_bitcast_fusion.3
  280.6 1.7 convolution_bitcast_fusion.3
  284.5 1.7 convolution_bitcast_fusion.3
  288.3 1.7 convolution_bitcast_fusion.3
  292.1 1.7 convolution_bitcast_fusion.3
  295.9 1.7 convolution_bitcast_fusion.3
  297.6 1.2 fusion.64
  299.7 1.7 convolution_bitcast_fusion.3
  303.5 4.0 %slice_bitcast_fusion.2 = (bf16[32,128,1,1,256]{4,1,3,2,0:T(8,128)(2,1)S(1)}, bf16[32,128,1,1,256]{4,1,3,2,0:T(8,128)(2,1)}) fusion(bf16[32,256,1,1,256]{4,1,0,3,2:T(8,128)(2,1)} %bitcast.189), kind=kLoop, calls=%fused_computation.64 | loop fusion | bytes 8388608 | tf_op jit(solution)/shard_map/split | solution.py:55
  307.5 33.1 %all_to_all.34 = bf16[32,128,1,1,256]{4,1,3,2,0:T(8,128)(2,1)} all-to-all(bf16[32,128,1,1,256]{4,1,3,2,0:T(8,128)(2,1)S(1)} %get-tuple-element.328), channel_id=1, replica_groups=mesh['seq'=4,'head'=32] {'head'}, dimensions={0} | all-to-all | bytes 4194304 | tf_op jit(solution)/shard_map/all_to_all | solution.py:57
  340.6 4.5 %all-to-all-start.3 = ((bf16[32,128,1,1,256]{4,1,3,2,0:T(8,128)(2,1)}), bf16[32,128,1,1,256]{4,1,3,2,0:T(8,128)(2,1)}, u32[]{:S(2)}, u32[]{:S(2)}) async-start(bf16[32,128,1,1,256]{4,1,3,2,0:T(8,128)(2,1)} %get-tuple-element.329), calls=%async_computation.3 | async-start | bytes 4194304 | tf_op jit(solution)/shard_map/all_to_all | solution.py:57
  345.2 6.4 %copy.71 = bf16[256,8192]{0,1:T(8,128)(2,1)} copy(bf16[256,8192]{1,0:T(8,128)(2,1)} %param.15) | data formatting | bytes 8388608 | tf_op args[4]
  351.6 3.2 copy.91
  354.8 18.8 %all-to-all-done.3 = bf16[32,128,1,1,256]{4,1,3,2,0:T(8,128)(2,1)} async-done(((bf16[32,128,1,1,256]{4,1,3,2,0:T(8,128)(2,1)}), bf16[32,128,1,1,256]{4,1,3,2,0:T(8,128)(2,1)}, u32[]{:S(2)}, u32[]{:S(2)}) %all-to-all-start.3) | async-done | bytes 2097184 | tf_op jit(solution)/shard_map/all_to_all | solution.py:57
  373.6 4.1 %copy.92 = bf16[32,128,1,1,256]{1,4,0,3,2:T(8,128)(2,1)} copy(bf16[32,128,1,1,256]{4,1,3,2,0:T(8,128)(2,1)} %all-to-all-done.3) | data formatting | bytes 4194304 | tf_op jit(solution)/shard_map/all_to_all | solution.py:57
  377.7 2.4 bitcast_reduce_fusion
  380.2 2.4 fusion.39
  382.7 6.2 %fusion.40 = bf16[256,8192]{0,1:T(8,128)(2,1)} fusion(bf16[256,8192]{0,1:T(8,128)(2,1)} %copy.71, f32[256,16]{0,1:T(8,128)S(1)} %add_sqrt_fusion, f32[256,16]{0,1:T(8,128)S(1)} %broadcast_multiply_fusion, bf16[32,128,1,1,256]{1,4,0,3,2:T(8,128)(2,1)} %copy.92, bf16[32,128,1,1,256]{1,4,0,3,2:T(8,128)(2,1)S(1)} %copy.91), kind=kLoop, calls=%fused_computation.52 | loop fusion | flops 27262976 | bytes 12615680 | tf_op jit(solution)/shard_map/convert_element_type | solution.py:192
  388.9 6.3 %copy.93 = bf16[256,8192]{1,0:T(8,128)(2,1)} copy(bf16[256,8192]{0,1:T(8,128)(2,1)} %fusion.40) | data formatting | bytes 8388608 | tf_op jit(solution)/shard_map/convert_element_type | solution.py:192
  (161 shorter events, 64.1 us)
Async XLA Ops:
  7.4 6.4 %copy-start.3 = (bf16[256,16]{0,1:T(8,128)(2,1)S(1)}, bf16[256,16]{0,1:T(8,128)(2,1)}, u32[]{:S(2)}) copy-start(bf16[256,16]{0,1:T(8,128)(2,1)} %param.14) | copy-start | bytes 24580
  13.8 2.8 copy-start.2
  143.7 7.5 %collective-permute-start = (bf16[8192,1,256]{2,0,1:T(8,128)(2,1)}, bf16[8192,1,256]{2,0,1:T(8,128)(2,1)}, u32[]{:S(2)}, u32[]{:S(2)}) collective-permute-start(bf16[8192,1,256]{2,0,1:T(8,128)(2,1)} %get-tuple-element.326), channel_id=1, source_target_pairs={{0,1},{1,0},{2,3},{3,2},{4,5},{5,4},{6,7},{7,6},{8,9},{9,8},{10,11... | collective-permute-start | bytes 12582920 | tf_op jit(solution)/shard_map/ppermute | solution.py:79
  149.6 6.8 %copy-start.1 = (bf16[8192,1,1,256]{3,0,2,1:T(8,128)(2,1)S(1)}, bf16[8192,1,1,256]{3,0,2,1:T(8,128)(2,1)}, u32[]{:S(2)}) copy-start(bf16[8192,1,1,256]{3,0,2,1:T(8,128)(2,1)} %get-tuple-element.327) | copy-start | bytes 12582916
  156.3 4.3 %copy-start = (bf16[8192,1,256]{2,0,1:T(8,128)(2,1)}, bf16[8192,1,256]{2,0,1:T(8,128)(2,1)S(1)}, u32[]{:S(2)}) copy-start(bf16[8192,1,256]{2,0,1:T(8,128)(2,1)S(1)} %get-tuple-element.324) | copy-start | bytes 12582916
  211.6 18.6 %all-to-all-start.1 = ((f32[4,1,1,65537]{3,2,1,0:T(1,128)}), f32[4,1,1,65537]{3,2,1,0:T(1,128)S(1)}, u32[]{:S(2)}, u32[]{:S(2)}) async-start(f32[4,1,1,65537]{3,2,1,0:T(1,128)} %broadcast_in_dim.46), calls=%async_computation.1 | async-start | bytes 2101248 | tf_op jit(solution)/shard_map/all_to_all | solution.py:13
  340.6 32.9 %all-to-all-start.3 = ((bf16[32,128,1,1,256]{4,1,3,2,0:T(8,128)(2,1)}), bf16[32,128,1,1,256]{4,1,3,2,0:T(8,128)(2,1)}, u32[]{:S(2)}, u32[]{:S(2)}) async-start(bf16[32,128,1,1,256]{4,1,3,2,0:T(8,128)(2,1)} %get-tuple-element.329), calls=%async_computation.3 | async-start | bytes 4194304 | tf_op jit(solution)/shard_map/all_to_all | solution.py:57
where the time goes:
time: 398 us; the launch traced here: 395 us
  blocking collectives  140 us (35%)
  local copies, waits for them, and re-layouts  90 us (23%)
  other arithmetic  68.5 us (17%)
  matrix products  51.1 us (13%)
  waiting for transfers between devices  34.8 us (9%)
  starting transfers between devices  8.95 us (2%)
    all_to_all x1, blocking collectives, side_by_side(): lax.all_to_all(both, axis, split_axis=split_dim, concat_axis=concat_dim,...  107 us
    all_to_all x1, blocking collectives, exchange_in_pieces(): lax.all_to_all(piece, axis, split_axis=0, concat_axis=0, tiled=True)  33.1 us
    dot_general x16, matrix products, emit_block(): jnp.einsum('nij,jnw->inw', weights, value_block, preferred_element_type=j...  27.2 us
    add x16, other arithmetic, advance(): jnp.exp(rate_row)[:, None, None] * carried_state + addition  26.7 us
    dot_general x16, matrix products, emit_block(): jnp.einsum('ind,ndw->inw', query_block, start_state.astype(jnp.bfloat16),...  19.6 us
    all_to_all x1, waiting for transfers between devices, exchange_in_pieces(): lax.all_to_all(piece, axis, split_axis=0, concat_axis=0, tiled=True)  18.8 us
    all_to_all x1, waiting for transfers between devices, sent_to_all(): lax.all_to_all(jnp.broadcast_to(shard[None], (count, *shard.shape)), axis...  14.4 us
    dynamic_update_slice x32, local copies, waits for them, and re-layouts, retain_items(): lax.map(emit_block, (query_blocks, key_blocks, value_blocks, running, sta...  13.7 us
  transfers between devices with their start and end apart: 3, of which 3 were waited for; matrix products, arithmetic and copies ran while one was open for 4% of the time, Pallas kernels for 0%

commit v1 on v0

v1 whole, which is shorter than its diff:
```python
import jax
import jax.numpy as jnp
from jax import lax
from jax.experimental import pallas as pl
from jax.experimental.pallas import tpu as pltpu
from jax.sharding import PartitionSpec as P

MESH = pl.DeviceIdType.MESH
HEADS = 16
NH = 8
DK = 256
DV = 512
BLOCK = 512
ROWS = 256
LINES = 16
F32 = jnp.float32
BF16 = jnp.bfloat16


def remote(src, dst, send_sem, recv_sem, device):
    return pltpu.make_async_remote_copy(
        src_ref=src,
        dst_ref=dst,
        send_sem=send_sem,
        recv_sem=recv_sem,
        device_id=device,
        device_id_type=MESH,
    )


def wide(row):
    return jnp.concatenate([row] * (DV // 128), axis=1)


def body(
    q_hbm, k_hbm, v_hbm, d_hbm, g_hbm, o_hbm,
    qs, ks, vs, gs, dl,
    fadeb, runb, erunb, runt,
    abuf, r1, bk, b2s, r2, bt, r3, tt, tb, c2s, cb, s1s, sb, within, obuf,
    l_own, l_z1, l_first, l_second, l_pair, l_z2, l_p0, l_p1, l_line, l_x,
    loc, d2s, d2r, dsem, lsem, ups, upr, xs, xr, osem,
):
    x = lax.axis_index("seq")
    hd = lax.axis_index("head")
    c = lax.rem(hd, 2)
    zy = lax.div(hd, 2)
    z = lax.rem(zy, 4)
    y = lax.div(zy, 4)
    zfirst = lax.rem(z, 2) == 0
    u = lax.rem(lax.div(z + 1, 2), 2)
    w = lax.div(z, 2)
    m = x * 4 + y
    partner = (x, hd + 1 - 2 * c)
    zp1 = (x, (y * 4 + z + 1 - 2 * lax.rem(z, 2)) * 2 + c)
    zp2 = (x, (y * 4 + 3 - z) * 2 + c)

    def line_device(line):
        return (lax.div(line, 4), (lax.rem(line, 4) * 4 + z) * 2 + c)

    def slot_of(line):
        return lax.rem(line - m + 2 * LINES - 1, LINES)

    my_rows = pl.ds(pl.multiple_of(c * ROWS, ROWS), ROWS)
    other_rows = pl.ds(pl.multiple_of((1 - c) * ROWS, ROWS), ROWS)
    half_mine = pl.ds(pl.multiple_of(u * 128, 128), 128)
    half_other = pl.ds(pl.multiple_of((1 - u) * 128, 128), 128)

    big = ((k_hbm, ks, DK), (v_hbm, vs, DV), (q_hbm, qs, DK), (g_hbm, gs, DV))

    def columns(core, h, width):
        return pl.ds(pl.multiple_of((core * NH + h) * width, width), width)

    def local_in(n, h):
        src, dst, width = big[n]
        return pltpu.make_async_copy(
            src.at[:, columns(c, h, width)], dst.at[h, my_rows], loc.at[n, h]
        )

    def cross_in(n, h):
        src, dst, width = big[n]
        return remote(
            src.at[:, columns(1 - c, h, width)],
            dst.at[h, my_rows],
            d2s.at[n, h],
            d2r.at[n, h],
            partner,
        )

    def cross_arrived(n, h):
        src, dst, width = big[n]
        remote(
            src.at[:, columns(c, h, width)],
            dst.at[h, other_rows],
            d2s.at[n, h],
            d2r.at[n, h],
            partner,
        ).wait_recv()

    d_local = pltpu.make_async_copy(d_hbm, dl.at[my_rows], dsem.at[0])
    d_cross = remote(d_hbm, dl.at[my_rows], dsem.at[1], dsem.at[2], partner)

    d_local.start()

    @pl.loop(0, NH)
    def _(h):
        for n in range(4):
            local_in(n, h).start()

    barrier = pltpu.get_barrier_semaphore()
    peers = [partner, zp1, zp2] + [line_device(lax.rem(m + k, LINES)) for k in range(1, LINES)]
    for peer in peers:
        pl.semaphore_signal(barrier, inc=1, device_id=peer, device_id_type=MESH)
    pl.semaphore_wait(barrier, len(peers))

    d_cross.start()

    @pl.loop(0, NH)
    def _(h):
        cross_in(0, h).start()
        cross_in(1, h).start()

    @pl.loop(0, NH)
    def _(h):
        cross_in(2, h).start()
        cross_in(3, h).start()

    d_local.wait()
    remote(d_hbm, dl.at[other_rows], dsem.at[1], dsem.at[2], partner).wait_recv()
    row = lax.broadcasted_iota(jnp.int32, (BLOCK, BLOCK), 0)
    col = lax.broadcasted_iota(jnp.int32, (BLOCK, BLOCK), 1)
    lower = jnp.where(row >= col, 1.0, 0.0).astype(BF16)
    upper = jnp.where(row <= col, 1.0, 0.0).astype(BF16)
    decays = dl[...]
    run16 = jnp.dot(lower, decays, preferred_element_type=F32)
    runt16 = lax.dot_general(
        decays, upper, (((0,), (0,)), ((), ())), preferred_element_type=F32
    )
    run8 = jnp.where(c == 0, run16[:, :NH], run16[:, NH:])
    runt8 = jnp.where(c == 0, runt16[:NH], runt16[NH:])
    runt[...] = runt8
    last = runt8[:, BLOCK - 1 : BLOCK]
    l_own[...] = jnp.broadcast_to(last, (NH, 128))
    fade8 = jnp.exp(run8[BLOCK - 1 : BLOCK] - run8)
    erun8 = jnp.exp(run8)
    for h in range(NH):
        fadeb[h] = jnp.broadcast_to(fade8[:, h : h + 1], (BLOCK, 128))
        runb[h] = jnp.broadcast_to(run8[:, h : h + 1], (BLOCK, 128))
        erunb[h] = jnp.broadcast_to(erun8[:, h : h + 1], (BLOCK, 128))

    l1_copy = remote(l_own, l_z1, lsem.at[0], lsem.at[1], zp1)
    l2_copy = remote(l_pair, l_z2, lsem.at[2], lsem.at[3], zp2)
    l1_copy.start()

    def up1(h):
        return remote(abuf.at[h, half_other], r1.at[h], ups.at[0, h], upr.at[0, h], zp1)

    def up2(h):
        return remote(b2s.at[h], r2.at[h], ups.at[1, h], upr.at[1, h], zp2)

    def down2(h, quarter):
        rows = pl.ds(pl.multiple_of(quarter * 64, 64), 64)
        return remote(c2s.at[h], cb.at[h, rows], ups.at[2, h], upr.at[2, h], zp2)

    def down1(h, rows):
        return remote(s1s.at[h], sb.at[h, rows], ups.at[3, h], upr.at[3, h], zp1)

    def x_send(h, k):
        line = lax.rem(m + k, LINES)
        return remote(
            bt.at[h, line],
            r3.at[h, LINES - 1 - k],
            xs.at[0, h],
            xr.at[0, h],
            line_device(line),
        )

    def y_send(h, k):
        line = lax.rem(m + k, LINES)
        return remote(
            tt.at[h, k - 1],
            tb.at[h, LINES - 1 - k],
            xs.at[1, h],
            xr.at[1, h],
            line_device(line),
        )

    def all_lines(buffer, n, h):
        some = buffer.at[h, pl.ds(0, LINES - 1)]
        return remote(some, some, xs.at[n, h], xr.at[n, h], zp1)

    @pl.loop(0, NH)
    def _(h):
        for n in range(2):
            local_in(n, h).wait()
            cross_arrived(n, h)
        fade = fadeb[h]
        faded = (ks[h].astype(F32) * jnp.concatenate([fade, fade], axis=1)).astype(BF16)
        addition = lax.dot_general(
            faded, vs[h], (((0,), (0,)), ((), ())), preferred_element_type=F32
        )
        abuf[h] = addition.astype(BF16)
        up1(h).start()

    l1_copy.wait_recv()
    mine, got = l_own[...], l_z1[...]
    l_first[...] = jnp.where(zfirst, mine, got)
    l_second[...] = jnp.where(zfirst, got, mine)
    l_pair[...] = mine + got
    l2_copy.start()

    def exp_row(ref, h):
        return jnp.exp(ref[pl.ds(h, 1), :])

    def combine_pair(h):
        up1(h).wait_recv()
        rate = wide(exp_row(l_second, h))
        one = jnp.ones_like(rate)
        rate_mine = jnp.where(zfirst, rate, one)
        rate_got = jnp.where(zfirst, one, rate)

        def total(quarter):
            at = pl.multiple_of(quarter * 64, 64)
            a = abuf[h, pl.ds(pl.multiple_of(u * 128 + at, 64), 64), :].astype(F32)
            b = r1[h, pl.ds(at, 64), :].astype(F32)
            return rate_mine * a + rate_got * b

        b2s[h] = total(1 - w).astype(BF16)
        up2(h).start()
        bk[h] = total(w)

    def share_rates():
        l2_copy.wait_recv()
        own_pair, got_pair = l_pair[...], l_z2[...]
        l_p0[...] = jnp.where(w == 0, own_pair, got_pair)
        l_p1[...] = jnp.where(w == 0, got_pair, own_pair)
        total = own_pair + got_pair
        l_line[...] = total
        l_x[LINES - 1] = total
        for k in range(1, LINES):
            remote(
                l_line,
                l_x.at[LINES - 1 - k],
                lsem.at[4],
                lsem.at[5],
                line_device(lax.rem(m + k, LINES)),
            ).start()

    rates_wait = remote(
        l_x.at[pl.ds(0, LINES - 1)], l_x.at[pl.ds(0, LINES - 1)], lsem.at[4], lsem.at[5], zp1
    )

    def combine_line(h):
        up2(h).wait_recv()
        rate = wide(exp_row(l_p1, h))
        one = jnp.ones_like(rate)
        total = jnp.where(w == 0, rate, one) * bk[h] + jnp.where(w == 0, one, rate) * r2[h].astype(F32)
        low = total.astype(BF16)
        for line in range(LINES):
            r, s = 16 * (line // 4), 128 * (line % 4)
            bt[h, line] = low[r : r + 16, s : s + 128]
        for k in range(1, LINES):
            x_send(h, k).start()
        r3[h, LINES - 1] = bt[h, m]

    def scan_lines(h):
        all_lines(r3, 0, h).wait_recv()
        carry = jnp.zeros((16, 128), F32)
        for line in range(LINES):
            slot = slot_of(line)
            low = carry.astype(BF16)
            tt[h, slot] = low
            if line < LINES - 1:
                rate = jnp.exp(l_x[slot, pl.ds(h, 1), :])
                carry = rate * carry + r3[h, slot].astype(F32)
        for k in range(1, LINES):
            y_send(h, k).start()
        tb[h, LINES - 1] = tt[h, LINES - 1]

    def carry_pairs(h):
        all_lines(tb, 1, h).wait_recv()
        rate = exp_row(l_p0, h)
        base = w * 64
        for line in range(LINES):
            r, s = 16 * (line // 4), 128 * (line % 4)
            start = tb[h, slot_of(line)].astype(F32)
            first_pair = jnp.where(
                w == 0, bk[h, r : r + 16, s : s + 128], r2[h, r : r + 16, s : s + 128].astype(F32)
            )
            after = rate * start + first_pair
            rows = pl.ds(pl.multiple_of(base + r, 16), 16)
            c2s[h, r : r + 16, s : s + 128] = jnp.where(w == 0, after, start).astype(BF16)
            cb[h, rows, s : s + 128] = jnp.where(w == 0, start, after).astype(BF16)
        down2(h, w).start()

    def carry_chips(h):
        down2(h, 1 - w).wait_recv()
        rate = wide(exp_row(l_first, h))
        for r in (0, 64):
            start = cb[h, r : r + 64, :].astype(F32)
            own_rows = pl.ds(pl.multiple_of(u * 128 + r, 64), 64)
            addition = jnp.where(zfirst, abuf[h, own_rows, :], r1[h, r : r + 64, :])
            after = rate * start + addition.astype(F32)
            s1s[h, r : r + 64, :] = jnp.where(zfirst, after, start).astype(BF16)
            sb[h, own_rows, :] = jnp.where(zfirst, start, after).astype(BF16)
        down1(h, half_mine).start()

    def within_block(h):
        local_in(2, h).wait()
        cross_arrived(2, h)
        for tile in range(2):
            keys = ROWS * (tile + 1)
            rows = slice(ROWS * tile, ROWS * (tile + 1))
            scores = lax.dot_general(
                qs[h, rows, :],
                ks[h, :keys, :],
                (((1,), (1,)), ((), ())),
                preferred_element_type=F32,
            )
            left = runb[h, rows, :]
            spread = jnp.concatenate([left] * (keys // 128), axis=1) - runt[pl.ds(h, 1), :keys]
            i = lax.broadcasted_iota(jnp.int32, (ROWS, keys), 0) + ROWS * tile
            j = lax.broadcasted_iota(jnp.int32, (ROWS, keys), 1)
            factor = jnp.exp(jnp.where(i >= j, spread, -jnp.inf))
            weights = (scores * factor).astype(BF16)
            within[h, rows, :] = jnp.dot(weights, vs[h, :keys, :], preferred_element_type=F32)

    def out_local(h):
        return pltpu.make_async_copy(
            obuf.at[h, my_rows], o_hbm.at[:, columns(c, h, DV)], osem.at[0, h]
        )

    def out_cross(h, core):
        return remote(
            obuf.at[h, other_rows],
            o_hbm.at[:, columns(core, h, DV)],
            osem.at[1, h],
            osem.at[2, h],
            partner,
        )

    def finish(h):
        local_in(3, h).wait()
        cross_arrived(3, h)
        down1(h, half_other).wait_recv()
        state = sb[h]
        for tile in range(4):
            rows = slice(128 * tile, 128 * (tile + 1))
            across = jnp.dot(qs[h, rows, :], state, preferred_element_type=F32)
            retained = within[h, rows, :] + across * wide(erunb[h, rows, :])
            retained = retained.astype(BF16).astype(F32)
            centered = retained - jnp.mean(retained, axis=1, keepdims=True)
            variance = jnp.mean(centered * centered, axis=1, keepdims=True)
            normed = centered * lax.rsqrt(variance + 1e-6)
            gate = gs[h, rows, :].astype(F32)
            gated = gate / (1.0 + jnp.exp(-gate)) * normed
            obuf[h, rows, :] = gated.astype(BF16)
        out_cross(h, c).start()
        out_local(h).start()

    @pl.loop(0, 2 * NH)
    def _(t):
        def stage(lag, f):
            @pl.when((t >= lag) & (t < lag + NH))
            def _():
                f(t - lag)

        stage(0, combine_pair)

        @pl.when(t == 0)
        def _():
            share_rates()

        stage(8, finish)
        stage(1, combine_line)
        stage(4, carry_pairs)
        stage(5, carry_chips)

        @pl.when(t == 2)
        def _():
            rates_wait.wait_recv()

        stage(2, scan_lines)
        stage(0, within_block)

    d_cross.wait_send()
    l1_copy.wait_send()
    l2_copy.wait_send()
    rates_wait.wait_send()

    @pl.loop(0, NH)
    def _(h):
        for n in range(4):
            cross_in(n, h).wait_send()
        up1(h).wait_send()
        up2(h).wait_send()
        down2(h, w).wait_send()
        down1(h, half_mine).wait_send()
        all_lines(r3, 0, h).wait_send()
        all_lines(tb, 1, h).wait_send()
        out_local(h).wait()
        out_cross(h, c).wait_send()
        out_cross(h, 1 - c).wait_recv()


def shards(queries, key_vectors, values, decay_log, gate_input):
    anywhere = pl.BlockSpec(memory_space=pl.ANY)
    tile = pltpu.VMEM((NH, 128), F32)
    dma = pltpu.SemaphoreType.DMA
    return pl.pallas_call(
        body,
        out_shape=jax.ShapeDtypeStruct((ROWS, HEADS * DV), BF16),
        in_specs=[anywhere] * 5,
        out_specs=anywhere,
        scratch_shapes=[
            pltpu.VMEM((NH, BLOCK, DK), BF16),
            pltpu.VMEM((NH, BLOCK, DK), BF16),
            pltpu.VMEM((NH, BLOCK, DV), BF16),
            pltpu.VMEM((NH, BLOCK, DV), BF16),
            pltpu.VMEM((BLOCK, HEADS), BF16),
            pltpu.VMEM((NH, BLOCK, 128), F32),
            pltpu.VMEM((NH, BLOCK, 128), F32),
            pltpu.VMEM((NH, BLOCK, 128), F32),
            pltpu.VMEM((NH, BLOCK), F32),
            pltpu.VMEM((NH, DK, DV), BF16),
            pltpu.VMEM((NH, 128, DV), BF16),
            pltpu.VMEM((NH, 64, DV), F32),
            pltpu.VMEM((NH, 64, DV), BF16),
            pltpu.VMEM((NH, 64, DV), BF16),
            pltpu.VMEM((NH, LINES, 16, 128), BF16),
            pltpu.VMEM((NH, LINES, 16, 128), BF16),
            pltpu.VMEM((NH, LINES, 16, 128), BF16),
            pltpu.VMEM((NH, LINES, 16, 128), BF16),
            pltpu.VMEM((NH, 64, DV), BF16),
            pltpu.VMEM((NH, 128, DV), BF16),
            pltpu.VMEM((NH, 128, DV), BF16),
            pltpu.VMEM((NH, DK, DV), BF16),
            pltpu.VMEM((NH, BLOCK, DV), F32),
            pltpu.VMEM((NH, BLOCK, DV), BF16),
            *[tile] * 9,
            pltpu.VMEM((LINES, NH, 128), F32),
            dma((4, NH)),
            dma((4, NH)),
            dma((4, NH)),
            dma((3,)),
            dma((6,)),
            dma((4, NH)),
            dma((4, NH)),
            dma((2, NH)),
            dma((2, NH)),
            dma((3, NH)),
        ],
        compiler_params=pltpu.CompilerParams(
            collective_id=0, has_side_effects=True, vmem_limit_bytes=60 * 1024 * 1024
        ),
        name="retention",
    )(queries, key_vectors, values, decay_log, gate_input)


def solution(mesh):
    spec = P(("seq", "head"), None)
    return jax.shard_map(
        shards, mesh=mesh, in_specs=(spec,) * 5, out_specs=spec, check_vma=False
    )
```

time: 398 us -> 70.3 us (0.18)
  blocking collectives: 140 us -> 0 us
  local copies, waits for them, and re-layouts: 90 us -> 6.07 us
  other arithmetic: 68.5 us -> 0 us
  Pallas kernels: 0 us -> 64 us
  matrix products: 51.1 us -> 0 us
  waiting for transfers between devices: 34.8 us -> 0 us
  starting transfers between devices: 8.95 us -> 0 us
    all_to_all x2 -> x0, blocking collectives: 140 us -> none  [the longest x1 107 us: side_by_side(): lax.all_to_all(both, axis, split_axis=split_dim, concat_axis=concat_dim,...]
    pallas_call x0 -> x1, Pallas kernels: none -> 64 us  [shards(): pl.pallas_call(body, out_shape=jax.ShapeDtypeStruct((ROWS, HEADS * DV), B...]
    dot_general x33 -> x0, matrix products: 51.1 us -> none  [the longest x16 27.2 us: emit_block(): jnp.einsum('nij,jnw->inw', weights, value_block, preferred_element_type=j...]
    all_to_all x2 -> x0, waiting for transfers between devices: 33.2 us -> none  [the longest x1 18.8 us: exchange_in_pieces(): lax.all_to_all(piece, axis, split_axis=0, concat_axis=0, tiled=True)]
    add x17 -> x0, other arithmetic: 29.4 us -> none  [the longest x16 26.7 us: advance(): jnp.exp(rate_row)[:, None, None] * carried_state + addition]
    all_to_all x3 -> x0, local copies, waits for them, and re-layouts: 20.8 us -> none  [the longest x1 13.5 us: side_by_side(): lax.all_to_all(both, axis, split_axis=split_dim, concat_axis=concat_dim,...]
    dynamic_update_slice x32 -> x0, local copies, waits for them, and re-layouts: 13.7 us -> none  [retain_items(): lax.map(emit_block, (query_blocks, key_blocks, value_blocks, running, sta...]
    dynamic_update_slice x16 -> x0, other arithmetic: 11.7 us -> none  [retain_items(): closing, local_starts = lax.scan(advance, initial, (block_decay, additions))]
  transfers between devices with their start and end apart: 3 -> 0, of which waited for: 3 -> 0; matrix products, arithmetic and copies ran while one was open for 4% -> 0% of each run, Pallas kernels for 0% -> 0%
where the time goes in v1:
time: 70.3 us; the launch traced here: 70.1 us
  Pallas kernels  64 us (91%)
  local copies, waits for them, and re-layouts  6.07 us (9%)
    pallas_call x1, Pallas kernels, shards(): pl.pallas_call(body, out_shape=jax.ShapeDtypeStruct((ROWS, HEADS * DV), B...  64 us
    unnamed x2, local copies, waits for them, and re-layouts  6.07 us

profile of v1, /device:TPU:1, one launch (start us, length us, event | category | flops | bytes accessed | tf_op | source)
XLA Modules:
  0.0 70.1 jit_solution(6948316341234651666)
XLA Ops:
  0.0 1.4 %copy.6.d_hbm = bf16[256,16]{1,0:T(8,128)(2,1)} copy(bf16[256,16]{0,1:T(8,128)(2,1)} %param.8) | data formatting | bytes 16384 | tf_op args[3]
  1.4 64.0 %retention.1 = bf16[256,8192]{1,0:T(8,128)(2,1)} custom-call(bf16[256,4096]{1,0:T(8,128)(2,1)} %q_hbm.1, bf16[256,4096]{1,0:T(8,128)(2,1)} %k_hbm.1, bf16[256,8192]{1,0:T(8,128)(2,1)} %v_hbm.1, bf16[256,16]{1,0:T(8,128)(2,1)} %copy.6.d_hbm, bf16[256,8192]{1,0:T(8,128)(2,1)} %g_hbm.1), custom_call_target="tpu_custom_call" | custom-call | tf_op jit(solution)/shard_map/retention/pallas_call | solution.py:409
  65.5 4.6 %copy.8 = bf16[256,8192]{1,0:T(8,128)(2,1)} copy(bf16[256,8192]{1,0:T(8,128)(2,1)} %retention.1) | data formatting | bytes 8388608

commit v2 on v1

--- a/solution.py
+++ b/solution.py
@@ -15,6 +15,7 @@
 LINES = 16
 F32 = jnp.float32
 BF16 = jnp.bfloat16
+VMEM = 52 * 1024 * 1024
 
 
 def remote(src, dst, send_sem, recv_sem, device):
@@ -96,8 +97,8 @@
             partner,
         ).wait_recv()
 
-    d_local = pltpu.make_async_copy(d_hbm, dl.at[my_rows], dsem.at[0])
-    d_cross = remote(d_hbm, dl.at[my_rows], dsem.at[1], dsem.at[2], partner)
+    d_local = pltpu.make_async_copy(d_hbm, dl.at[:, my_rows], dsem.at[0])
+    d_cross = remote(d_hbm, dl.at[:, my_rows], dsem.at[1], dsem.at[2], partner)
 
     d_local.start()
 
@@ -125,16 +126,16 @@
         cross_in(3, h).start()
 
     d_local.wait()
-    remote(d_hbm, dl.at[other_rows], dsem.at[1], dsem.at[2], partner).wait_recv()
+    remote(d_hbm, dl.at[:, other_rows], dsem.at[1], dsem.at[2], partner).wait_recv()
     row = lax.broadcasted_iota(jnp.int32, (BLOCK, BLOCK), 0)
     col = lax.broadcasted_iota(jnp.int32, (BLOCK, BLOCK), 1)
     lower = jnp.where(row >= col, 1.0, 0.0).astype(BF16)
     upper = jnp.where(row <= col, 1.0, 0.0).astype(BF16)
     decays = dl[...]
-    run16 = jnp.dot(lower, decays, preferred_element_type=F32)
-    runt16 = lax.dot_general(
-        decays, upper, (((0,), (0,)), ((), ())), preferred_element_type=F32
+    run16 = lax.dot_general(
+        lower, decays, (((1,), (1,)), ((), ())), preferred_element_type=F32
     )
+    runt16 = jnp.dot(decays, upper, preferred_element_type=F32)
     run8 = jnp.where(c == 0, run16[:, :NH], run16[:, NH:])
     runt8 = jnp.where(c == 0, runt16[:NH], runt16[NH:])
     runt[...] = runt8
@@ -357,7 +358,7 @@
         out_cross(h, c).start()
         out_local(h).start()
 
-    @pl.loop(0, 2 * NH)
+    @pl.loop(0, NH + 8)
     def _(t):
         def stage(lag, f):
             @pl.when((t >= lag) & (t < lag + NH))
@@ -370,16 +371,16 @@
         def _():
             share_rates()
 
+        stage(6, carry_chips)
+
+        @pl.when(t == 3)
+        def _():
+            rates_wait.wait_recv()
+
+        stage(3, scan_lines)
         stage(8, finish)
         stage(1, combine_line)
         stage(4, carry_pairs)
-        stage(5, carry_chips)
-
-        @pl.when(t == 2)
-        def _():
-            rates_wait.wait_recv()
-
-        stage(2, scan_lines)
         stage(0, within_block)
 
     d_cross.wait_send()
@@ -408,15 +409,15 @@
     dma = pltpu.SemaphoreType.DMA
     return pl.pallas_call(
         body,
-        out_shape=jax.ShapeDtypeStruct((ROWS, HEADS * DV), BF16),
+        out_shape=pltpu.VMEM((ROWS, HEADS * DV), BF16),
         in_specs=[anywhere] * 5,
-        out_specs=anywhere,
+        out_specs=pl.BlockSpec(memory_space=pltpu.VMEM),
         scratch_shapes=[
             pltpu.VMEM((NH, BLOCK, DK), BF16),
             pltpu.VMEM((NH, BLOCK, DK), BF16),
             pltpu.VMEM((NH, BLOCK, DV), BF16),
             pltpu.VMEM((NH, BLOCK, DV), BF16),
-            pltpu.VMEM((BLOCK, HEADS), BF16),
+            pltpu.VMEM((HEADS, BLOCK), BF16),
             pltpu.VMEM((NH, BLOCK, 128), F32),
             pltpu.VMEM((NH, BLOCK, 128), F32),
             pltpu.VMEM((NH, BLOCK, 128), F32),
@@ -450,10 +451,10 @@
             dma((3, NH)),
         ],
         compiler_params=pltpu.CompilerParams(
-            collective_id=0, has_side_effects=True, vmem_limit_bytes=60 * 1024 * 1024
+            collective_id=0, has_side_effects=True, vmem_limit_bytes=VMEM
         ),
         name="retention",
-    )(queries, key_vectors, values, decay_log, gate_input)
+    )(queries, key_vectors, values, decay_log.T, gate_input)
 
 
 def solution(mesh):

time: 70.3 us -> 65.1 us (0.926)
  local copies, waits for them, and re-layouts: 6.07 us -> 2.02 us
  Pallas kernels: 64 us -> 63 us
    unnamed x2 -> x1, local copies, waits for them, and re-layouts: 6.07 us -> 2.02 us
    pallas_call x1, Pallas kernels: 64 us -> 63 us  [shards(): pl.pallas_call(body, out_shape=pltpu.VMEM((ROWS, HEADS * DV), BF16), in_s...]
where the time goes in v2:
time: 65.1 us; the launch traced here: 65 us
  Pallas kernels  63 us (97%)
  local copies, waits for them, and re-layouts  2.02 us (3%)
    pallas_call x1, Pallas kernels, shards(): pl.pallas_call(body, out_shape=pltpu.VMEM((ROWS, HEADS * DV), BF16), in_s...  63 us
    unnamed x1, local copies, waits for them, and re-layouts  2.02 us

profile of v2, /device:TPU:1, one launch (start us, length us, event | category | flops | bytes accessed | tf_op | source)
XLA Modules:
  0.0 65.0 jit_solution(5556694976115982690)
XLA Ops:
  0.0 63.0 %retention.1 = bf16[256,8192]{1,0:T(8,128)(2,1)S(1)} custom-call(bf16[256,4096]{1,0:T(8,128)(2,1)} %q_hbm.1, bf16[256,4096]{1,0:T(8,128)(2,1)} %k_hbm.1, bf16[256,8192]{1,0:T(8,128)(2,1)} %v_hbm.1, bf16[16,256]{1,0:T(8,128)(2,1)} %bitcast.1, bf16[256,8192]{1,0:T(8,128)(2,1)} %g_hbm.1), custom_call_target="tpu_custom_call" | custom-call | tf_op jit(solution)/shard_map/retention/pallas_call | solution.py:410
  63.0 2.0 %copy.7 = bf16[256,8192]{1,0:T(8,128)(2,1)} copy(bf16[256,8192]{1,0:T(8,128)(2,1)S(1)} %retention.1) | data formatting | bytes 8388608

commit v3 on v2

--- a/solution.py
+++ b/solution.py
@@ -34,7 +34,7 @@
 
 
 def body(
-    q_hbm, k_hbm, v_hbm, d_hbm, g_hbm, o_hbm,
+    q_hbm, k_hbm, v_hbm, d_hbm, g_hbm, o_ref,
     qs, ks, vs, gs, dl,
     fadeb, runb, erunb, runt,
     abuf, r1, bk, b2s, r2, bt, r3, tt, tb, c2s, cb, s1s, sb, within, obuf,
@@ -71,10 +71,13 @@
     def columns(core, h, width):
         return pl.ds(pl.multiple_of((core * NH + h) * width, width), width)
 
+    def arrival(sems, n, h):
+        return sems.at[n, h] if n < 2 else sems.at[n, 0]
+
     def local_in(n, h):
         src, dst, width = big[n]
         return pltpu.make_async_copy(
-            src.at[:, columns(c, h, width)], dst.at[h, my_rows], loc.at[n, h]
+            src.at[:, columns(c, h, width)], dst.at[h, my_rows], arrival(loc, n, h)
         )
 
     def cross_in(n, h):
@@ -82,20 +85,19 @@
         return remote(
             src.at[:, columns(1 - c, h, width)],
             dst.at[h, my_rows],
-            d2s.at[n, h],
-            d2r.at[n, h],
+            d2s.at[n],
+            arrival(d2r, n, h),
             partner,
         )
 
     def cross_arrived(n, h):
-        src, dst, width = big[n]
-        remote(
-            src.at[:, columns(c, h, width)],
-            dst.at[h, other_rows],
-            d2s.at[n, h],
-            d2r.at[n, h],
-            partner,
-        ).wait_recv()
+        dst = big[n][1].at[h, other_rows]
+        remote(dst, dst, d2s.at[n], arrival(d2r, n, h), partner).wait_recv()
+
+    def all_arrived(n):
+        own, got = big[n][1].at[:, my_rows], big[n][1].at[:, other_rows]
+        pltpu.make_async_copy(own, own, loc.at[n, 0]).wait()
+        remote(got, got, d2s.at[n], d2r.at[n, 0], partner).wait_recv()
 
     d_local = pltpu.make_async_copy(d_hbm, dl.at[:, my_rows], dsem.at[0])
     d_cross = remote(d_hbm, dl.at[:, my_rows], dsem.at[1], dsem.at[2], partner)
@@ -104,7 +106,7 @@
 
     @pl.loop(0, NH)
     def _(h):
-        for n in range(4):
+        for n in range(2):
             local_in(n, h).start()
 
     barrier = pltpu.get_barrier_semaphore()
@@ -122,8 +124,9 @@
 
     @pl.loop(0, NH)
     def _(h):
-        cross_in(2, h).start()
-        cross_in(3, h).start()
+        for n in (2, 3):
+            local_in(n, h).start()
+            cross_in(n, h).start()
 
     d_local.wait()
     remote(d_hbm, dl.at[:, other_rows], dsem.at[1], dsem.at[2], partner).wait_recv()
@@ -153,24 +156,24 @@
     l1_copy.start()
 
     def up1(h):
-        return remote(abuf.at[h, half_other], r1.at[h], ups.at[0, h], upr.at[0, h], zp1)
+        return remote(abuf.at[h, half_other], r1.at[h], ups.at[0], upr.at[0, h], zp1)
 
     def up2(h):
-        return remote(b2s.at[h], r2.at[h], ups.at[1, h], upr.at[1, h], zp2)
+        return remote(b2s.at[h], r2.at[h], ups.at[1], upr.at[1, h], zp2)
 
     def down2(h, quarter):
         rows = pl.ds(pl.multiple_of(quarter * 64, 64), 64)
-        return remote(c2s.at[h], cb.at[h, rows], ups.at[2, h], upr.at[2, h], zp2)
+        return remote(c2s.at[h], cb.at[h, rows], ups.at[2], upr.at[2, h], zp2)
 
     def down1(h, rows):
-        return remote(s1s.at[h], sb.at[h, rows], ups.at[3, h], upr.at[3, h], zp1)
+        return remote(s1s.at[h], sb.at[h, rows], ups.at[3], upr.at[3, h], zp1)
 
     def x_send(h, k):
         line = lax.rem(m + k, LINES)
         return remote(
             bt.at[h, line],
             r3.at[h, LINES - 1 - k],
-            xs.at[0, h],
+            xs.at[0],
             xr.at[0, h],
             line_device(line),
         )
@@ -180,14 +183,14 @@
         return remote(
             tt.at[h, k - 1],
             tb.at[h, LINES - 1 - k],
-            xs.at[1, h],
+            xs.at[1],
             xr.at[1, h],
             line_device(line),
         )
 
     def all_lines(buffer, n, h):
         some = buffer.at[h, pl.ds(0, LINES - 1)]
-        return remote(some, some, xs.at[n, h], xr.at[n, h], zp1)
+        return remote(some, some, xs.at[n], xr.at[n, h], zp1)
 
     @pl.loop(0, NH)
     def _(h):
@@ -306,8 +309,10 @@
         down1(h, half_mine).start()
 
     def within_block(h):
-        local_in(2, h).wait()
-        cross_arrived(2, h)
+        @pl.when(h == 0)
+        def _():
+            all_arrived(2)
+
         for tile in range(2):
             keys = ROWS * (tile + 1)
             rows = slice(ROWS * tile, ROWS * (tile + 1))
@@ -325,27 +330,21 @@
             weights = (scores * factor).astype(BF16)
             within[h, rows, :] = jnp.dot(weights, vs[h, :keys, :], preferred_element_type=F32)
 
-    def out_local(h):
-        return pltpu.make_async_copy(
-            obuf.at[h, my_rows], o_hbm.at[:, columns(c, h, DV)], osem.at[0, h]
-        )
-
     def out_cross(h, core):
         return remote(
-            obuf.at[h, other_rows],
-            o_hbm.at[:, columns(core, h, DV)],
-            osem.at[1, h],
-            osem.at[2, h],
-            partner,
+            obuf.at[h], o_ref.at[:, columns(core, h, DV)], osem.at[0], osem.at[1], partner
         )
 
     def finish(h):
-        local_in(3, h).wait()
-        cross_arrived(3, h)
+        @pl.when(h == 0)
+        def _():
+            all_arrived(3)
+
         down1(h, half_other).wait_recv()
         state = sb[h]
-        for tile in range(4):
-            rows = slice(128 * tile, 128 * (tile + 1))
+
+        def gated_rows(first, tile):
+            rows = pl.ds(pl.multiple_of(first * ROWS + 128 * tile, 128), 128)
             across = jnp.dot(qs[h, rows, :], state, preferred_element_type=F32)
             retained = within[h, rows, :] + across * wide(erunb[h, rows, :])
             retained = retained.astype(BF16).astype(F32)
@@ -353,10 +352,13 @@
             variance = jnp.mean(centered * centered, axis=1, keepdims=True)
             normed = centered * lax.rsqrt(variance + 1e-6)
             gate = gs[h, rows, :].astype(F32)
-            gated = gate / (1.0 + jnp.exp(-gate)) * normed
-            obuf[h, rows, :] = gated.astype(BF16)
+            return (gate / (1.0 + jnp.exp(-gate)) * normed).astype(BF16)
+
+        for tile in range(2):
+            obuf[h, 128 * tile : 128 * (tile + 1), :] = gated_rows(1 - c, tile)
         out_cross(h, c).start()
-        out_local(h).start()
+        for tile in range(2):
+            o_ref[128 * tile : 128 * (tile + 1), columns(c, h, DV)] = gated_rows(c, tile)
 
     @pl.loop(0, NH + 8)
     def _(t):
@@ -388,19 +390,20 @@
     l2_copy.wait_send()
     rates_wait.wait_send()
 
-    @pl.loop(0, NH)
-    def _(h):
-        for n in range(4):
-            cross_in(n, h).wait_send()
-        up1(h).wait_send()
-        up2(h).wait_send()
-        down2(h, w).wait_send()
-        down1(h, half_mine).wait_send()
-        all_lines(r3, 0, h).wait_send()
-        all_lines(tb, 1, h).wait_send()
-        out_local(h).wait()
-        out_cross(h, c).wait_send()
-        out_cross(h, 1 - c).wait_recv()
+    def all_sent(ref, sem):
+        remote(ref, ref, sem, osem.at[1], partner).wait_send()
+
+    for n in range(4):
+        all_sent(big[n][1].at[:, my_rows], d2s.at[n])
+    all_sent(r1, ups.at[0])
+    all_sent(r2, ups.at[1])
+    all_sent(c2s, ups.at[2])
+    all_sent(s1s, ups.at[3])
+    all_sent(r3.at[:, pl.ds(0, LINES - 1)], xs.at[0])
+    all_sent(tb.at[:, pl.ds(0, LINES - 1)], xs.at[1])
+    all_sent(obuf, osem.at[0])
+    others = o_ref.at[:, pl.ds(pl.multiple_of((1 - c) * NH * DV, NH * DV), NH * DV)]
+    remote(others, others, osem.at[0], osem.at[1], partner).wait_recv()
 
 
 def shards(queries, key_vectors, values, decay_log, gate_input):
@@ -436,19 +439,19 @@
             pltpu.VMEM((NH, 128, DV), BF16),
             pltpu.VMEM((NH, DK, DV), BF16),
             pltpu.VMEM((NH, BLOCK, DV), F32),
-            pltpu.VMEM((NH, BLOCK, DV), BF16),
+            pltpu.VMEM((NH, ROWS, DV), BF16),
             *[tile] * 9,
             pltpu.VMEM((LINES, NH, 128), F32),
             dma((4, NH)),
-            dma((4, NH)),
+            dma((4,)),
             dma((4, NH)),
             dma((3,)),
             dma((6,)),
+            dma((4,)),
             dma((4, NH)),
-            dma((4, NH)),
+            dma((2,)),
             dma((2, NH)),
-            dma((2, NH)),
-            dma((3, NH)),
+            dma((2,)),
         ],
         compiler_params=pltpu.CompilerParams(
             collective_id=0, has_side_effects=True, vmem_limit_bytes=VMEM

time: 65.1 us -> 64 us (0.983)
  Pallas kernels: 63 us -> 61.9 us
    pallas_call x1, Pallas kernels: 63 us -> 61.9 us  [shards(): pl.pallas_call(body, out_shape=pltpu.VMEM((ROWS, HEADS * DV), BF16), in_s...]
where the time goes in v3:
time: 64 us; the launch traced here: 63.9 us
  Pallas kernels  61.9 us (97%)
  local copies, waits for them, and re-layouts  2.02 us (3%)
    pallas_call x1, Pallas kernels, shards(): pl.pallas_call(body, out_shape=pltpu.VMEM((ROWS, HEADS * DV), BF16), in_s...  61.9 us
    unnamed x1, local copies, waits for them, and re-layouts  2.02 us

profile of v3, /device:TPU:1, one launch (start us, length us, event | category | flops | bytes accessed | tf_op | source)
XLA Modules:
  0.0 63.9 jit_solution(17569786398658649312)
XLA Ops:
  0.0 61.9 %retention.1 = bf16[256,8192]{1,0:T(8,128)(2,1)S(1)} custom-call(bf16[256,4096]{1,0:T(8,128)(2,1)} %q_hbm.1, bf16[256,4096]{1,0:T(8,128)(2,1)} %k_hbm.1, bf16[256,8192]{1,0:T(8,128)(2,1)} %v_hbm.1, bf16[16,256]{1,0:T(8,128)(2,1)} %bitcast.1, bf16[256,8192]{1,0:T(8,128)(2,1)} %g_hbm.1), custom_call_target="tpu_custom_call" | custom-call | tf_op jit(solution)/shard_map/retention/pallas_call | solution.py:413
  61.9 2.0 %copy.7 = bf16[256,8192]{1,0:T(8,128)(2,1)} copy(bf16[256,8192]{1,0:T(8,128)(2,1)S(1)} %retention.1) | data formatting | bytes 8388608

commit v4 on v3

--- a/solution.py
+++ b/solution.py
@@ -36,7 +36,7 @@
 def body(
     q_hbm, k_hbm, v_hbm, d_hbm, g_hbm, o_ref,
     qs, ks, vs, gs, dl,
-    fadeb, runb, erunb, runt,
+    runb, erunb, runt,
     abuf, r1, bk, b2s, r2, bt, r3, tt, tb, c2s, cb, s1s, sb, within, obuf,
     l_own, l_z1, l_first, l_second, l_pair, l_z2, l_p0, l_p1, l_line, l_x,
     loc, d2s, d2r, dsem, lsem, ups, upr, xs, xr, osem,
@@ -102,6 +102,11 @@
     d_local = pltpu.make_async_copy(d_hbm, dl.at[:, my_rows], dsem.at[0])
     d_cross = remote(d_hbm, dl.at[:, my_rows], dsem.at[1], dsem.at[2], partner)
 
+    barrier = pltpu.get_barrier_semaphore()
+    peers = [partner, zp1, zp2] + [line_device(lax.rem(m + k, LINES)) for k in range(1, LINES)]
+    for peer in peers:
+        pl.semaphore_signal(barrier, inc=1, device_id=peer, device_id_type=MESH)
+
     d_local.start()
 
     @pl.loop(0, NH)
@@ -109,10 +114,6 @@
         for n in range(2):
             local_in(n, h).start()
 
-    barrier = pltpu.get_barrier_semaphore()
-    peers = [partner, zp1, zp2] + [line_device(lax.rem(m + k, LINES)) for k in range(1, LINES)]
-    for peer in peers:
-        pl.semaphore_signal(barrier, inc=1, device_id=peer, device_id_type=MESH)
     pl.semaphore_wait(barrier, len(peers))
 
     d_cross.start()
@@ -122,38 +123,25 @@
         cross_in(0, h).start()
         cross_in(1, h).start()
 
-    @pl.loop(0, NH)
-    def _(h):
-        for n in (2, 3):
-            local_in(n, h).start()
-            cross_in(n, h).start()
-
-    d_local.wait()
-    remote(d_hbm, dl.at[:, other_rows], dsem.at[1], dsem.at[2], partner).wait_recv()
     row = lax.broadcasted_iota(jnp.int32, (BLOCK, BLOCK), 0)
     col = lax.broadcasted_iota(jnp.int32, (BLOCK, BLOCK), 1)
     lower = jnp.where(row >= col, 1.0, 0.0).astype(BF16)
     upper = jnp.where(row <= col, 1.0, 0.0).astype(BF16)
+    d_local.wait()
+    remote(d_hbm, dl.at[:, other_rows], dsem.at[1], dsem.at[2], partner).wait_recv()
     decays = dl[...]
+    runt16 = jnp.dot(decays, upper, preferred_element_type=F32)
     run16 = lax.dot_general(
         lower, decays, (((1,), (1,)), ((), ())), preferred_element_type=F32
     )
-    runt16 = jnp.dot(decays, upper, preferred_element_type=F32)
+    runt8 = jnp.where(c == 0, runt16[:NH], runt16[NH:])
+    l_own[...] = jnp.broadcast_to(runt8[:, BLOCK - 1 : BLOCK], (NH, 128))
+    runt[...] = runt8
     run8 = jnp.where(c == 0, run16[:, :NH], run16[:, NH:])
-    runt8 = jnp.where(c == 0, runt16[:NH], runt16[NH:])
-    runt[...] = runt8
-    last = runt8[:, BLOCK - 1 : BLOCK]
-    l_own[...] = jnp.broadcast_to(last, (NH, 128))
     fade8 = jnp.exp(run8[BLOCK - 1 : BLOCK] - run8)
-    erun8 = jnp.exp(run8)
-    for h in range(NH):
-        fadeb[h] = jnp.broadcast_to(fade8[:, h : h + 1], (BLOCK, 128))
-        runb[h] = jnp.broadcast_to(run8[:, h : h + 1], (BLOCK, 128))
-        erunb[h] = jnp.broadcast_to(erun8[:, h : h + 1], (BLOCK, 128))
 
     l1_copy = remote(l_own, l_z1, lsem.at[0], lsem.at[1], zp1)
     l2_copy = remote(l_pair, l_z2, lsem.at[2], lsem.at[3], zp2)
-    l1_copy.start()
 
     def up1(h):
         return remote(abuf.at[h, half_other], r1.at[h], ups.at[0], upr.at[0, h], zp1)
@@ -192,18 +180,28 @@
         some = buffer.at[h, pl.ds(0, LINES - 1)]
         return remote(some, some, xs.at[n], xr.at[n, h], zp1)
 
-    @pl.loop(0, NH)
-    def _(h):
+    l1_copy.start()
+    for h in range(NH):
         for n in range(2):
             local_in(n, h).wait()
             cross_arrived(n, h)
-        fade = fadeb[h]
-        faded = (ks[h].astype(F32) * jnp.concatenate([fade, fade], axis=1)).astype(BF16)
+        fade = jnp.broadcast_to(fade8[:, h : h + 1], (BLOCK, DK))
+        faded = (ks[h].astype(F32) * fade).astype(BF16)
         addition = lax.dot_general(
             faded, vs[h], (((0,), (0,)), ((), ())), preferred_element_type=F32
         )
         abuf[h] = addition.astype(BF16)
         up1(h).start()
+
+    @pl.loop(0, NH)
+    def _(h):
+        local_in(2, h).start()
+        cross_in(2, h).start()
+
+    @pl.loop(0, NH)
+    def _(h):
+        local_in(3, h).start()
+        cross_in(3, h).start()
 
     l1_copy.wait_recv()
     mine, got = l_own[...], l_z1[...]
@@ -211,6 +209,11 @@
     l_second[...] = jnp.where(zfirst, got, mine)
     l_pair[...] = mine + got
     l2_copy.start()
+
+    erun8 = jnp.exp(run8)
+    for h in range(NH):
+        runb[h] = jnp.broadcast_to(run8[:, h : h + 1], (BLOCK, 128))
+        erunb[h] = jnp.broadcast_to(erun8[:, h : h + 1], (BLOCK, 128))
 
     def exp_row(ref, h):
         return jnp.exp(ref[pl.ds(h, 1), :])
@@ -383,7 +386,7 @@
         stage(8, finish)
         stage(1, combine_line)
         stage(4, carry_pairs)
-        stage(0, within_block)
+        stage(3, within_block)
 
     d_cross.wait_send()
     l1_copy.wait_send()
@@ -421,7 +424,6 @@
             pltpu.VMEM((NH, BLOCK, DV), BF16),
             pltpu.VMEM((NH, BLOCK, DV), BF16),
             pltpu.VMEM((HEADS, BLOCK), BF16),
-            pltpu.VMEM((NH, BLOCK, 128), F32),
             pltpu.VMEM((NH, BLOCK, 128), F32),
             pltpu.VMEM((NH, BLOCK, 128), F32),
             pltpu.VMEM((NH, BLOCK), F32),

time: 64 us -> 62.7 us (0.980)
  Pallas kernels: 61.9 us -> 60.6 us
    pallas_call x1, Pallas kernels: 61.9 us -> 60.6 us  [shards(): pl.pallas_call(body, out_shape=pltpu.VMEM((ROWS, HEADS * DV), BF16), in_s...]
where the time goes in v4:
time: 62.7 us; the launch traced here: 62.6 us
  Pallas kernels  60.6 us (97%)
  local copies, waits for them, and re-layouts  2.02 us (3%)
    pallas_call x1, Pallas kernels, shards(): pl.pallas_call(body, out_shape=pltpu.VMEM((ROWS, HEADS * DV), BF16), in_s...  60.6 us
    unnamed x1, local copies, waits for them, and re-layouts  2.02 us

profile of v4, /device:TPU:1, one launch (start us, length us, event | category | flops | bytes accessed | tf_op | source)
XLA Modules:
  0.0 62.6 jit_solution(17687270895264781114)
XLA Ops:
  0.0 60.6 %retention.1 = bf16[256,8192]{1,0:T(8,128)(2,1)S(1)} custom-call(bf16[256,4096]{1,0:T(8,128)(2,1)} %q_hbm.1, bf16[256,4096]{1,0:T(8,128)(2,1)} %k_hbm.1, bf16[256,8192]{1,0:T(8,128)(2,1)} %v_hbm.1, bf16[16,256]{1,0:T(8,128)(2,1)} %bitcast.1, bf16[256,8192]{1,0:T(8,128)(2,1)} %g_hbm.1), custom_call_target="tpu_custom_call" | custom-call | tf_op jit(solution)/shard_map/retention/pallas_call | solution.py:416
  60.6 2.0 %copy.7 = bf16[256,8192]{1,0:T(8,128)(2,1)} copy(bf16[256,8192]{1,0:T(8,128)(2,1)S(1)} %retention.1) | data formatting | bytes 8388608

commit v5 on v4

--- a/solution.py
+++ b/solution.py
@@ -333,9 +333,14 @@
             weights = (scores * factor).astype(BF16)
             within[h, rows, :] = jnp.dot(weights, vs[h, :keys, :], preferred_element_type=F32)
 
-    def out_cross(h, core):
+    def out_cross(h, core, tile):
+        rows = pl.ds(128 * tile, 128)
         return remote(
-            obuf.at[h], o_ref.at[:, columns(core, h, DV)], osem.at[0], osem.at[1], partner
+            obuf.at[h, rows],
+            o_ref.at[rows, columns(core, h, DV)],
+            osem.at[0],
+            osem.at[1],
+            partner,
         )
 
     def finish(h):
@@ -359,7 +364,7 @@
 
         for tile in range(2):
             obuf[h, 128 * tile : 128 * (tile + 1), :] = gated_rows(1 - c, tile)
-        out_cross(h, c).start()
+            out_cross(h, c, tile).start()
         for tile in range(2):
             o_ref[128 * tile : 128 * (tile + 1), columns(c, h, DV)] = gated_rows(c, tile)
 

time: 62.7 us -> 63 us (level)
  no operation moved by 1% of the time
where the time goes in v5:
time: 63 us; the launch traced here: 62.9 us
  Pallas kernels  60.9 us (97%)
  local copies, waits for them, and re-layouts  2.02 us (3%)
    pallas_call x1, Pallas kernels, shards(): pl.pallas_call(body, out_shape=pltpu.VMEM((ROWS, HEADS * DV), BF16), in_s...  60.9 us
    unnamed x1, local copies, waits for them, and re-layouts  2.02 us

profile of v5, /device:TPU:1, one launch (start us, length us, event | category | flops | bytes accessed | tf_op | source)
XLA Modules:
  0.0 62.9 jit_solution(17524908464077221260)
XLA Ops:
  0.0 60.9 %retention.1 = bf16[256,8192]{1,0:T(8,128)(2,1)S(1)} custom-call(bf16[256,4096]{1,0:T(8,128)(2,1)} %q_hbm.1, bf16[256,4096]{1,0:T(8,128)(2,1)} %k_hbm.1, bf16[256,8192]{1,0:T(8,128)(2,1)} %v_hbm.1, bf16[16,256]{1,0:T(8,128)(2,1)} %bitcast.1, bf16[256,8192]{1,0:T(8,128)(2,1)} %g_hbm.1), custom_call_target="tpu_custom_call" | custom-call | tf_op jit(solution)/shard_map/retention/pallas_call | solution.py:421
  60.9 2.0 %copy.7 = bf16[256,8192]{1,0:T(8,128)(2,1)} copy(bf16[256,8192]{1,0:T(8,128)(2,1)S(1)} %retention.1) | data formatting | bytes 8388608
